TPU v7x, 256 devices: a 2x2x32 block of a 4x8x32 slice. The times are simulated.
256 devices in a mesh: groups: 4 (over x, y), ctx: 64 (over z, core).
Axes of the slice: x: 2, y: 2, z: 32, core: 2. Of those that a mesh axis runs over, the one named last changes fastest.
The devices are a block of a 4x8x32 slice.
Arguments:
- queries: bfloat16 [32768, 1024], P(('groups', 'ctx')), parts along dimension 0, may hold values from -27 to 27
- keys: bfloat16 [32768, 1024], P(('groups', 'ctx')), parts along dimension 0, may hold values from -6 to 6
- values: bfloat16 [32768, 1024], P(('groups', 'ctx')), parts along dimension 0, may hold values from -6 to 6
- resid: bfloat16 [32768, 2048], P(('groups', 'ctx')), parts along dimension 0, may hold values from -6 to 6
- out_proj: bfloat16 [1024, 2048], replicated, may hold values from -0.1875 to 0.1875
- norm_gain: float32 [2048], replicated, may hold values from 0.25 to 1.75
- up_proj: bfloat16 [2048, 4096], P(None, 'ctx'), may hold values from -0.125 to 0.125
- down_proj: bfloat16 [2048, 4096], P(None, 'ctx'), may hold values from -0.09375 to 0.09375
- router: bfloat16 [2048, 8], replicated, may hold values from -0.125 to 0.125
- expert_ids: int32 [32768, 1], P(('groups', 'ctx')), parts along dimension 0, may hold values from 0 to 7; in each aligned block of 128 rows (0 to 127, 128 to 255, ...) at most 20 rows name the same one
- expert_in: bfloat16 [64, 2048, 512], P('ctx'), may hold values from -0.125 to 0.125
- expert_out: bfloat16 [64, 512, 2048], P('ctx'), may hold values from -0.09375 to 0.09375
Outputs:
- layer_out: bfloat16 [32768, 2048], P(('groups', 'ctx')), parts along dimension 0
There are 4 independent parts, one for each index of `groups`. A program takes and returns all parts, laid end to end along the dimension named above; an argument that names none is the same for every part. Nothing has to cross between parts.
Inputs may be any that keep to these rules, and one draw needn't show every extreme that they name: `expert_ids`: among the 128 tokens of one index of ctx, at most 20 name the same expert; in every draw some index of ctx has 20 tokens naming one expert.
All inputs are finite; a program needn't handle non-finite values.
Results may differ from a plain program's by a relative error of at most 0.0075.
Values may be sent and summed in bfloat16 or wider, within the bound.
A program may use at most 192 MiB of HBM per device.

v0:
```python
import jax
import jax.numpy as jnp
from jax import lax
from jax.sharding import PartitionSpec as P

DH = 128
SPLIT = 8


NEG_FILL = -1e30
EPSILON = 1e-06


def in_one_piece(arrays, axis, dim, along):
    ends, at = ([], 0)
    for a in arrays[:-1]:
        at += a.shape[along]
        ends.append(at)
    both = jnp.concatenate(arrays, axis=along)
    return tuple(jnp.split(lax.all_gather(both, axis, axis=dim, tiled=True), ends, axis=along))


def from_partner(array, axis, apart):
    return lax.ppermute(array, axis, [(i, i ^ 1 << apart) for i in range(lax.axis_size(axis))])


def update_state(state, query_rows, query_offset, key_block, value_block, key_offset):
    maxima, totals, numer = state
    count_query = query_rows.shape[0]
    count_keys = key_block.shape[0]
    head_count = query_rows.shape[1] // DH
    query_heads = query_rows.reshape(count_query, head_count, DH)
    key_heads = key_block.reshape(count_keys, head_count, DH)
    value_heads = value_block.reshape(count_keys, head_count, DH)
    scores = jnp.einsum(
        "qhd,khd->hqk", query_heads, key_heads, preferred_element_type=jnp.float32
    ) * DH ** (-0.5)
    query_positions = query_offset + jnp.arange(count_query, dtype=jnp.int32)
    key_positions = key_offset + jnp.arange(count_keys, dtype=jnp.int32)
    visible = (key_positions[None, :] <= query_positions[:, None])[None]
    masked = jnp.where(visible, scores, NEG_FILL)
    new_max = jnp.maximum(maxima, jnp.max(masked, axis=2))
    weights = jnp.where(visible, jnp.exp(masked - new_max[..., None]), 0.0)
    factor = jnp.exp(maxima - new_max)
    totals = totals * factor + jnp.sum(weights, axis=2)
    numer = numer * factor[..., None] + jnp.einsum(
        "hqk,khd->hqd",
        weights.astype(jnp.bfloat16),
        value_heads,
        preferred_element_type=jnp.float32,
    )
    return (new_max, totals, numer)


def attend(query_sets, keys, values):
    head_count = keys.shape[1] // DH
    initial = []
    for query_rows, query_offset in query_sets:
        count_query = query_rows.shape[0]
        initial.append(
            (
                jnp.full((head_count, count_query), NEG_FILL, jnp.float32),
                jnp.zeros((head_count, count_query), jnp.float32),
                jnp.zeros((head_count, count_query, DH), jnp.float32),
            )
        )
    states = tuple(initial)
    key_offset = jnp.int32(0)
    key_whole, value_whole = in_one_piece((keys, values), "ctx", 0, 1)
    total_keys = key_whole.shape[0]
    step_rows = min(total_keys, 1024)
    for begin in range(0, total_keys, step_rows):
        key_block = key_whole[begin : begin + step_rows]
        value_block = value_whole[begin : begin + step_rows]
        block_offset = key_offset + begin
        query_rows, query_offset = query_sets[0]
        needed = block_offset <= query_offset + query_rows.shape[0] - 1
        updated = [
            lax.cond(
                needed,
                lambda carried, rows_now=query_rows, offset_now=query_offset, keys_now=key_block, values_now=value_block, start_now=block_offset: update_state(
                    carried, rows_now, offset_now, keys_now, values_now, start_now
                ),
                lambda carried: carried,
                states[0],
            )
        ]
        states = tuple(updated)
    results = []
    for maxima, totals, numer in states:
        result = (numer / totals[..., None]).astype(jnp.bfloat16)
        results.append(
            jnp.transpose(result, (1, 0, 2)).reshape(result.shape[1], result.shape[0] * DH)
        )
    return results


def body(
    queries,
    keys,
    values,
    resid,
    out_proj,
    norm_gain,
    up_proj,
    down_proj,
    router,
    expert_ids,
    expert_in,
    expert_out,
):
    tok_rows = queries.shape[0]
    width = resid.shape[1]
    live_count = router.shape[1]
    ctx_count = lax.axis_size("ctx")
    device_index = lax.axis_index("ctx")
    base_offset = device_index * tok_rows
    attn = attend([(queries, base_offset)], keys, values)[0]
    mixed = resid.astype(jnp.float32) + jnp.dot(attn, out_proj, preferred_element_type=jnp.float32)
    normed = (
        mixed * lax.rsqrt(jnp.mean(mixed * mixed, axis=1, keepdims=True) + EPSILON) * norm_gain
    ).astype(jnp.bfloat16)
    mlp_blocks = jnp.stack([up_proj, down_proj], 0)
    for level in range(live_count.bit_length() - 1):
        other_block = from_partner(mlp_blocks, "ctx", level)
        mlp_blocks = jnp.concatenate([mlp_blocks, other_block], axis=2)
    slots_per = max(2, 5 * tok_rows // (4 * live_count))
    chosen = expert_ids[:, 0]
    onehot = (chosen[:, None] == jnp.arange(live_count, dtype=jnp.int32)[None, :]).astype(
        jnp.bfloat16
    )
    row_iota = jnp.arange(tok_rows, dtype=jnp.int32)
    strictly_lower = (row_iota[None, :] < row_iota[:, None]).astype(jnp.bfloat16)
    counts_before = jnp.dot(strictly_lower, onehot, preferred_element_type=jnp.float32)
    slot_index = jnp.sum(onehot.astype(jnp.float32) * counts_before, axis=1).astype(jnp.int32)
    target_slot = chosen * slots_per + slot_index
    dispatch_matrix = (
        jnp.arange(live_count * slots_per, dtype=jnp.int32)[:, None] == target_slot[None, :]
    ).astype(jnp.bfloat16)
    packed = jnp.dot(dispatch_matrix, normed, preferred_element_type=jnp.float32).astype(
        jnp.bfloat16
    )
    sending = jnp.broadcast_to(
        packed.reshape(1, live_count, slots_per, width), (SPLIT, live_count, slots_per, width)
    )
    sending = sending.reshape(ctx_count, 1, slots_per, width)
    own_expert = device_index % live_count
    router_column = lax.dynamic_slice_in_dim(router, own_expert, 1, 1)
    weight_in = expert_in[0]
    weight_out = expert_out[0]
    received = lax.all_to_all(sending, "ctx", split_axis=0, concat_axis=1, tiled=True)
    rows = received.reshape(-1, width)
    expert_hidden = jax.nn.gelu(
        jnp.dot(rows, weight_in, preferred_element_type=jnp.float32)
    ).astype(jnp.bfloat16)
    mlp_hidden = jax.nn.gelu(
        jnp.dot(rows, mlp_blocks[0], preferred_element_type=jnp.float32)
    ).astype(jnp.bfloat16)
    gate = jax.nn.sigmoid(jnp.dot(rows, router_column, preferred_element_type=jnp.float32))
    produced = gate * jnp.dot(expert_hidden, weight_out, preferred_element_type=jnp.float32)
    produced = produced + lax.dot_general(
        mlp_hidden, mlp_blocks[1], (((1,), (1,)), ((), ())), preferred_element_type=jnp.float32
    )
    came_back = lax.all_to_all(
        produced.astype(jnp.bfloat16).reshape(received.shape),
        "ctx",
        split_axis=1,
        concat_axis=0,
        tiled=True,
    )
    summed = jnp.sum(
        came_back.astype(jnp.float32).reshape(SPLIT, live_count * slots_per, width), axis=0
    )
    mixture_part = lax.dot_general(
        dispatch_matrix.astype(jnp.float32),
        summed,
        (((0,), (0,)), ((), ())),
        preferred_element_type=jnp.float32,
    )
    return (mixed + mixture_part).astype(jnp.bfloat16)


def solution(mesh):
    placed = (
        P(("groups", "ctx"), None),
        P(("groups", "ctx"), None),
        P(("groups", "ctx"), None),
        P(("groups", "ctx"), None),
        P(),
        P(),
        P(None, "ctx"),
        P(None, "ctx"),
        P(),
        P(("groups", "ctx"), None),
        P("ctx", None, None),
        P("ctx", None, None),
    )
    return jax.shard_map(
        body, mesh=mesh, in_specs=placed, out_specs=P(("groups", "ctx"), None), check_vma=False
    )
```

profile of v0, /device:TPU:38, one launch (start us, length us, event | category | flops | bytes accessed | tf_op | source)
XLA Modules:
  0.0 1698.1 jit_solution(5593962587991613827)
XLA Ops:
  11.4 266.9 %all-gather.2.cloned.1.call-done = bf16[8192,2048]{0,1:T(8,128)(2,1)} async-done(((bf16[128,2048]{0,1:T(8,128)(2,1)}), bf16[8192,2048]{0,1:T(8,128)(2,1)}) %all-gather.2.cloned.1.call-update) | async-done | bytes 33554448 | tf_op jit(solution)/shard_map/all_gather | solution.py:20
  278.3 17.3 %fusion.196 = (bf16[1024,1024]{0,1:T(8,128)(2,1)}, bf16[1024,1024]{0,1:T(8,128)(2,1)}, bf16[1024,1024]{0,1:T(8,128)(2,1)}, bf16[1024,1024]{0,1:T(8,128)(2,1)}, b...) fusion(bf16[8192,2048]{0,1:T(8,128)(2,1)} %all-gather.2.cloned., ...), kind=kLoop, calls=%fused_computation.247 | loop fusion | bytes 50331648 | tf_op jit(solution)/shard_map/slice | solution.py:74
  295.7 6.9 conditional.8
  300.2 2.3 fusion.10
  303.1 6.1 conditional.13
  309.2 7.2 conditional.15
  316.5 3.1 multiply_reduce_fusion
  320.9 2.0 broadcast_in_dim.187
  322.9 4.6 broadcast_in_dim.188
  327.5 55.4 %all-to-all-start = ((bf16[64,1,20,2048]{3,2,1,0:T(8,128)(2,1)}), bf16[64,1,20,2048]{3,2,1,0:T(8,128)(2,1)}, u32[]{:S(2)}, u32[]{:S(2)}) async-start(bf16[64,1,20,2048]{3,2,1,0:T(8,128)(2,1)} %bitcast.141), calls=%async_computation | async-start | bytes 12582912 | tf_op jit(solution)/shard_map/all_to_all | solution.py:151
  388.0 557.5 %collective-permute-done.1 = bf16[2,2048,128]{1,2,0:T(8,128)(2,1)S(1)} collective-permute-done((bf16[2,2048,128]{1,2,0:T(8,128)(2,1)S(1)}, bf16[2,2048,128]{1,2,0:T(8,128)(2,1)S(1)}, u32[]{:S(2)}, u32[]{:S(2)}) %collective-permute-start.1) | collective-permute-done | bytes 1048608 | tf_op jit(solution)/shard_map/ppermute | solution.py:24
  945.5 2.7 pad_maximum_fusion.1
  948.2 2.7 collective-permute-start.2
  950.9 90.8 %collective-permute-done.2 = bf16[2,2048,256]{1,2,0:T(8,128)(2,1)} collective-permute-done((bf16[2,2048,256]{1,2,0:T(8,128)(2,1)}, bf16[2,2048,256]{1,2,0:T(8,128)(2,1)}, u32[]{:S(2)}, u32[]{:S(2)}) %collective-permute-start.2) | collective-permute-done | bytes 2097184 | tf_op jit(solution)/shard_map/ppermute | solution.py:24
  1041.6 3.7 pad_maximum_fusion
  1045.3 9.0 reshape.419
  1054.3 4.0 convolution_reduce_fusion
  1058.3 11.0 fusion.171
  1069.3 12.3 add_convert_fusion
  1081.6 8.9 reshape.421
  1090.5 582.2 %all_to_all.8 = bf16[1,64,20,2048]{3,2,0,1:T(8,128)(2,1)} all-to-all(bf16[1,64,20,2048]{3,2,0,1:T(8,128)(2,1)} %bitcast.142), channel_id=1, replica_groups=mesh['groups'=4,'ctx'=64] {'ctx'}, dimensions={1} | all-to-all | bytes 10485760 | tf_op jit(solution)/shard_map/all_to_all | solution.py:164
  1672.7 9.8 reshape.422
  1682.5 6.0 reduce_sum.101
  1688.6 2.2 fusion.169
  (41 shorter events, 16.5 us)
Async XLA Ops:
  6.5 1051.8 %copy-start = (bf16[1,512,2048]{2,1,0:T(8,128)(2,1)S(1)}, bf16[1,512,2048]{2,1,0:T(8,128)(2,1)}, u32[]{:S(2)}) copy-start(bf16[1,512,2048]{2,1,0:T(8,128)(2,1)} %param.39) | copy-start | bytes 6291460
  6.6 271.8 %all-gather.2.cloned.1.call-start = ((), (), s32[]{:S(2)}) async-start(), calls=%async_computation.2 | async-start | bytes 34078720 | tf_op jit(solution)/shard_map/all_gather | solution.py:20
  11.4 284.2 %copy-start.1 = (bf16[128,1024]{1,0:T(8,128)(2,1)S(1)}, bf16[128,1024]{1,0:T(8,128)(2,1)}, u32[]{:S(2)}) copy-start(bf16[128,1024]{1,0:T(8,128)(2,1)} %param.28) | copy-start | bytes 786436
  316.4 3.2 copy-start.10
  327.5 55.4 %copy-start.3 = (bf16[2048,64]{0,1:T(8,128)(2,1)S(1)}, bf16[2048,64]{0,1:T(8,128)(2,1)}, u32[]{:S(2)}) copy-start(bf16[2048,64]{0,1:T(8,128)(2,1)} %param.35) | copy-start | bytes 786436
  327.5 717.8 %all-to-all-start = ((bf16[64,1,20,2048]{3,2,1,0:T(8,128)(2,1)}), bf16[64,1,20,2048]{3,2,1,0:T(8,128)(2,1)}, u32[]{:S(2)}, u32[]{:S(2)}) async-start(bf16[64,1,20,2048]{3,2,1,0:T(8,128)(2,1)} %bitcast.141), calls=%async_computation | async-start | bytes 12582912 | tf_op jit(solution)/shard_map/all_to_all | solution.py:151
  384.0 2.0 collective-permute-start
  386.0 559.5 %copy-start.2 = (bf16[2,2048,64]{1,2,0:T(8,128)(2,1)}, bf16[2,2048,64]{1,2,0:T(8,128)(2,1)S(1)}, u32[]{:S(2)}) copy-start(bf16[2,2048,64]{1,2,0:T(8,128)(2,1)S(1)} %collective-permute-done) | copy-start | bytes 1572868
  387.2 558.3 %collective-permute-start.1 = (bf16[2,2048,128]{1,2,0:T(8,128)(2,1)S(1)}, bf16[2,2048,128]{1,2,0:T(8,128)(2,1)S(1)}, u32[]{:S(2)}, u32[]{:S(2)}) collective-permute-start(bf16[2,2048,128]{1,2,0:T(8,128)(2,1)S(1)} %pad_maximum_fusion.2), channel_id=1, source_target_pairs={{0,2},{1,3},{2,0},{3,1},{4,6},{5,7},{6,4},{7,5},{8,10},{9,11},{10,... | collective-permute-start | bytes 3145736 | tf_op jit(solution)/shard_map/ppermute | solution.py:24
  945.5 2.7 copy-start.4
  948.2 93.5 %collective-permute-start.2 = (bf16[2,2048,256]{1,2,0:T(8,128)(2,1)}, bf16[2,2048,256]{1,2,0:T(8,128)(2,1)}, u32[]{:S(2)}, u32[]{:S(2)}) collective-permute-start(bf16[2,2048,256]{1,2,0:T(8,128)(2,1)} %pad_maximum_fusion.1), channel_id=1, source_target_pairs={{0,4},{1,5},{2,6},{3,7},{4,0},{5,1},{6,2},{7,3},{8,12},{9,13},{10,... | collective-permute-start | bytes 6291464 | tf_op jit(solution)/shard_map/ppermute | solution.py:24
Sparse Core Ops, SparseCore 0:
  10.0 268.3 all-gather.1
where the time goes:
time: 1710 us; the launch traced here: 1700 us
  waiting for transfers between devices  917 us (54%)
  blocking collectives  582 us (34%)
  starting transfers between devices  59.1 us (3%)
  local copies, waits for them, and re-layouts  54.2 us (3%)
  matrix products  38.1 us (2%)
  other arithmetic  19.6 us (1%)
    ppermute x3, waiting for transfers between devices, from_partner(): lax.ppermute(array, axis, [(i, i ^ 1 << apart) for i in range(lax.axis_si...  650 us
    all_to_all x1, blocking collectives, body(): lax.all_to_all(produced.astype(jnp.bfloat16).reshape(received.shape), 'ct...  582 us
    all_gather x1, waiting for transfers between devices, in_one_piece(): lax.all_gather(both, axis, axis=dim, tiled=True)  267 us
    all_to_all x1, starting transfers between devices, body(): lax.all_to_all(sending, 'ctx', split_axis=0, concat_axis=1, tiled=True)  55.4 us
  transfers between devices with their start and end apart: 5, of which 4 were waited for; matrix products, arithmetic and copies ran while one was open for 1% of the time, Pallas kernels for 0%

commit v1 on v0

v1 whole, which is shorter than its diff:
```python
import functools
import jax
import jax.numpy as jnp
from jax import lax
from jax.experimental import pallas as pl
from jax.experimental.pallas import tpu as pltpu
from jax.sharding import PartitionSpec as P

DH = 128
SPLIT = 8
NEG_FILL = -1e30
EPSILON = 1e-06
LOG2E = 1.4426950408889634
KEY_BLOCK = 1024
QUERY_BLOCK = 256


def attend_kernel(members, tok_rows, q_ref, k_ref, v_ref, o_ref):
    pair = pl.program_id(0)
    member = lax.rem(lax.axis_index("ctx"), members)
    q = q_ref[...]
    segment = members * tok_rows
    scale = DH ** (-0.5) * LOG2E

    def block(begin, carry, masked):
        best, total, numer = carry
        keys = k_ref[pl.ds(begin, KEY_BLOCK), :]
        values = v_ref[pl.ds(begin, KEY_BLOCK), :]
        s = lax.dot_general(q, keys, (((1,), (1,)), ((), ())), preferred_element_type=jnp.float32)
        s = s * scale
        if masked:
            row = lax.broadcasted_iota(jnp.int32, s.shape, 0) + pair * QUERY_BLOCK
            at = (row // tok_rows) * segment + member * tok_rows + row % tok_rows
            key_at = lax.broadcasted_iota(jnp.int32, s.shape, 1) + begin
            s = jnp.where(key_at <= at, s, NEG_FILL)
        new_best = jnp.maximum(best, jnp.max(s, axis=1, keepdims=True))
        p = jnp.exp2(s - new_best)
        factor = jnp.exp2(best - new_best)
        total = total * factor + jnp.sum(p, axis=1, keepdims=True)
        numer = numer * factor + jnp.dot(
            p.astype(jnp.bfloat16), values, preferred_element_type=jnp.float32
        )
        return new_best, total, numer

    carry = (
        jnp.full((QUERY_BLOCK, 1), NEG_FILL, jnp.float32),
        jnp.zeros((QUERY_BLOCK, 1), jnp.float32),
        jnp.zeros((QUERY_BLOCK, DH), jnp.float32),
    )
    per_block = QUERY_BLOCK // tok_rows * segment // KEY_BLOCK
    carry = lax.fori_loop(
        0,
        pair * per_block,
        lambda i, c: block(pl.multiple_of(i * KEY_BLOCK, KEY_BLOCK), c, False),
        carry,
    )
    for extra in range(per_block):
        carry = block(
            pl.multiple_of((pair * per_block + extra) * KEY_BLOCK, KEY_BLOCK), carry, True
        )
    _, total, numer = carry
    o_ref[...] = (numer / total).astype(o_ref.dtype)


def attend(q, k, v, members, tok_rows):
    rows = q.shape[0]
    whole = pl.BlockSpec(k.shape, lambda i: (0, 0))
    return pl.pallas_call(
        functools.partial(attend_kernel, members, tok_rows),
        out_shape=jax.ShapeDtypeStruct(q.shape, jnp.bfloat16),
        grid=(rows // QUERY_BLOCK,),
        in_specs=[pl.BlockSpec((QUERY_BLOCK, DH), lambda i: (i, 0)), whole, whole],
        out_specs=pl.BlockSpec((QUERY_BLOCK, DH), lambda i: (i, 0)),
        cost_estimate=pl.CostEstimate(flops=10**10, bytes_accessed=5 * 10**6, transcendentals=5 * 10**6),
    )(q, k, v)


def body(
    queries,
    keys,
    values,
    resid,
    out_proj,
    norm_gain,
    up_proj,
    down_proj,
    router,
    expert_ids,
    expert_in,
    expert_out,
):
    tok_rows = queries.shape[0]
    heads = queries.shape[1] // DH
    width = resid.shape[1]
    live_count = router.shape[1]
    ctx_count = lax.axis_size("ctx")
    members = ctx_count // heads
    device_index = lax.axis_index("ctx")
    across = [[h * members + m for h in range(heads)] for m in range(members)]
    within = [[h * members + m for m in range(members)] for h in range(heads)]

    mlp_piece = jnp.stack([up_proj.T, down_proj.T], 0)
    qkv = jnp.stack([queries, keys, values], 0).reshape(3, tok_rows, heads, DH)
    qkv = jnp.transpose(qkv, (2, 0, 1, 3))
    mine = lax.all_to_all(
        qkv, "ctx", split_axis=0, concat_axis=0, tiled=True, axis_index_groups=across
    )
    q = mine[:, 0].reshape(heads * tok_rows, DH)
    kv = lax.all_gather(mine[:, 1:], "ctx", axis=0, axis_index_groups=within)
    k = jnp.transpose(kv[:, :, 0], (1, 0, 2, 3)).reshape(-1, DH)
    v = jnp.transpose(kv[:, :, 1], (1, 0, 2, 3)).reshape(-1, DH)
    mlp = lax.all_gather(mlp_piece, "ctx", axis=0, axis_index_groups=within)
    up_t = mlp[:, 0].reshape(-1, width)
    down_t = mlp[:, 1].reshape(-1, width)

    o = attend(q, k, v, members, tok_rows).reshape(heads, tok_rows, DH)
    o = lax.all_to_all(
        o, "ctx", split_axis=0, concat_axis=0, tiled=True, axis_index_groups=across
    )
    attn = jnp.transpose(o, (1, 0, 2)).reshape(tok_rows, heads * DH)

    mixed = resid.astype(jnp.float32) + jnp.dot(attn, out_proj, preferred_element_type=jnp.float32)
    normed = (
        mixed * lax.rsqrt(jnp.mean(mixed * mixed, axis=1, keepdims=True) + EPSILON) * norm_gain
    ).astype(jnp.bfloat16)

    slots_per = max(2, 5 * tok_rows // (4 * live_count))
    chosen = expert_ids[:, 0]
    onehot = (chosen[:, None] == jnp.arange(live_count, dtype=jnp.int32)[None, :]).astype(
        jnp.bfloat16
    )
    row_iota = jnp.arange(tok_rows, dtype=jnp.int32)
    strictly_lower = (row_iota[None, :] < row_iota[:, None]).astype(jnp.bfloat16)
    counts_before = jnp.dot(strictly_lower, onehot, preferred_element_type=jnp.float32)
    slot_index = jnp.sum(onehot.astype(jnp.float32) * counts_before, axis=1).astype(jnp.int32)
    target_slot = chosen * slots_per + slot_index
    own_expert = device_index % live_count
    all_slots = lax.all_gather(target_slot, "ctx", axis=0)
    tokens = lax.all_gather(normed, "ctx", axis=0)
    select = (
        all_slots[:, None, :]
        == (own_expert * slots_per + jnp.arange(slots_per, dtype=jnp.int32))[None, :, None]
    ).astype(jnp.bfloat16)
    rows = (
        jnp.einsum("jst,jtw->jsw", select, tokens, preferred_element_type=jnp.float32)
        .astype(jnp.bfloat16)
        .reshape(-1, width)
    )
    router_column = lax.dynamic_slice_in_dim(router, own_expert, 1, 1)
    weight_in = expert_in[0]
    weight_out = expert_out[0]
    expert_hidden = jax.nn.gelu(
        jnp.dot(rows, weight_in, preferred_element_type=jnp.float32)
    ).astype(jnp.bfloat16)
    mlp_hidden = jax.nn.gelu(
        lax.dot_general(rows, up_t, (((1,), (1,)), ((), ())), preferred_element_type=jnp.float32)
    ).astype(jnp.bfloat16)
    gate = jax.nn.sigmoid(jnp.dot(rows, router_column, preferred_element_type=jnp.float32))
    produced = gate * jnp.dot(expert_hidden, weight_out, preferred_element_type=jnp.float32)
    produced = produced + jnp.dot(mlp_hidden, down_t, preferred_element_type=jnp.float32)
    produced = produced.astype(jnp.bfloat16).reshape(ctx_count, slots_per, width)
    spread = jnp.einsum("jst,jsw->jtw", select, produced, preferred_element_type=jnp.float32)
    spread = spread.astype(jnp.bfloat16).reshape(ctx_count * tok_rows, width)
    summed = lax.psum_scatter(spread, "ctx", scatter_dimension=0, tiled=True)
    return (mixed + summed.astype(jnp.float32)).astype(jnp.bfloat16)


def solution(mesh):
    placed = (
        P(("groups", "ctx"), None),
        P(("groups", "ctx"), None),
        P(("groups", "ctx"), None),
        P(("groups", "ctx"), None),
        P(),
        P(),
        P(None, "ctx"),
        P(None, "ctx"),
        P(),
        P(("groups", "ctx"), None),
        P("ctx", None, None),
        P("ctx", None, None),
    )
    return jax.shard_map(
        body, mesh=mesh, in_specs=placed, out_specs=P(("groups", "ctx"), None), check_vma=False
    )
```

time: 1710 us -> 817 us (0.48)
  waiting for transfers between devices: 917 us -> 457 us
  blocking collectives: 582 us -> 226 us
  starting transfers between devices: 59.1 us -> 0.2 us
  matrix products: 38.1 us -> 62.8 us
  local copies, waits for them, and re-layouts: 54.2 us -> 35.3 us
    ppermute x3 -> x0, waiting for transfers between devices: 650 us -> none  [from_partner(): lax.ppermute(array, axis, [(i, i ^ 1 << apart) for i in range(lax.axis_si...]
    all_to_all x1 -> x2, blocking collectives: 582 us -> 171 us  [the longest x1 108 us: body(): lax.all_to_all(qkv, 'ctx', split_axis=0, concat_axis=0, tiled=True, axis_...]
    reduce_scatter x0 -> x1, waiting for transfers between devices: none -> 259 us  [body(): summed = lax.psum_scatter(spread, 'ctx', scatter_dimension=0, tiled=True)]
    all_gather x1 -> x3, waiting for transfers between devices: 267 us -> 198 us  [the longest x1 142 us: body(): tokens = lax.all_gather(normed, 'ctx', axis=0)]
    all_gather x0 -> x1, blocking collectives: none -> 55.4 us  [body(): all_slots = lax.all_gather(target_slot, 'ctx', axis=0)]
    all_to_all x1 -> x0, starting transfers between devices: 55.4 us -> none  [body(): lax.all_to_all(sending, 'ctx', split_axis=0, concat_axis=1, tiled=True)]
    dot_general x5 -> x3, matrix products: 19.2 us -> 43.9 us  [the longest x1 16.5 us: body(): jnp.einsum('jst,jsw->jtw', select, produced, preferred_element_type=jnp.f...]
  transfers between devices with their start and end apart: 5 -> 4, of which waited for: 4 -> 3; matrix products, arithmetic and copies ran while one was open for 1% -> 2% of each run, Pallas kernels for 0% -> 2%
where the time goes in v1:
time: 817 us; the launch traced here: 816 us
  waiting for transfers between devices  457 us (56%)
  blocking collectives  226 us (28%)
  matrix products  62.8 us (8%)
  local copies, waits for them, and re-layouts  35.3 us (4%)
  Pallas kernels  16.2 us (2%)
  between operations  13.3 us (2%)
    reduce_scatter x1, waiting for transfers between devices, body(): summed = lax.psum_scatter(spread, 'ctx', scatter_dimension=0, tiled=True)  259 us
    all_gather x1, waiting for transfers between devices, body(): tokens = lax.all_gather(normed, 'ctx', axis=0)  142 us
    all_to_all x1, blocking collectives, body(): lax.all_to_all(qkv, 'ctx', split_axis=0, concat_axis=0, tiled=True, axis_...  108 us
    all_to_all x1, blocking collectives, body(): lax.all_to_all(o, 'ctx', split_axis=0, concat_axis=0, tiled=True, axis_in...  62.6 us
    all_gather x1, waiting for transfers between devices, body(): kv = lax.all_gather(mine[:, 1:], 'ctx', axis=0, axis_index_groups=within)  56.1 us
    all_gather x1, blocking collectives, body(): all_slots = lax.all_gather(target_slot, 'ctx', axis=0)  55.4 us
    dot_general x1, matrix products, body(): jnp.einsum('jst,jsw->jtw', select, produced, preferred_element_type=jnp.f...  16.5 us
  transfers between devices with their start and end apart: 4, of which 3 were waited for; matrix products, arithmetic and copies ran while one was open for 2% of the time, Pallas kernels for 2%

profile of v1, /device:TPU:38, one launch (start us, length us, event | category | flops | bytes accessed | tf_op | source)
XLA Modules:
  0.0 815.9 jit_solution(1162536489416574872)
XLA Ops:
  6.6 1.3 copy.36
  7.8 1.1 copy.37
  9.0 1.1 copy.38
  10.3 108.4 %all_to_all.10 = bf16[8,3,128,128]{2,3,1,0:T(8,128)(2,1)S(1)} all-to-all(bf16[8,3,128,128]{2,3,1,0:T(8,128)(2,1)S(1)} %copy.39), channel_id=1, replica_groups={{0,8,16,24,32,40,48,56},{1,9,17,25,33,41,49,57},{2,10,18,26,34,42,50,58..., dimensions={0} | all-to-all | bytes 1572864 | tf_op jit(solution)/shard_map/all_to_all | solution.py:105
  119.8 1.9 pad_maximum_fusion
  122.7 56.1 %all-gather.8.cloned.1.call-done = bf16[64,2,128,128]{3,2,1,0:T(8,128)(2,1)} async-done(((bf16[8,2,128,128]{3,2,1,0:T(8,128)(2,1)}), bf16[64,2,128,128]{3,2,1,0:T(8,128)(2,1)}) %all-gather.8.cloned.1.call-update) | async-done | bytes 4194320 | tf_op jit(solution)/shard_map/all_gather | solution.py:109
  178.8 2.7 slice_bitcast_fusion
  181.6 1.6 copy.43
  183.1 1.6 copy.42
  184.7 16.2 %shard_map.118 = bf16[1024,128]{1,0:T(8,128)(2,1)} custom-call(bf16[1024,128]{1,0:T(8,128)(2,1)} %bitcast.75, bf16[8192,128]{1,0:T(8,128)(2,1)} %bitcast.66, bf16[8192,128]{1,0:T(8,128)(2,1)} %bitcast.65), custom_call_target="tpu_custom_call" | custom-call | flops 10000000000 | bytes 5000000 | tf_op jit(solution)/shard_map/pallas_call | solution.py:68
  202.1 62.6 %all_to_all.11 = bf16[8,128,128]{1,2,0:T(8,128)(2,1)S(1)} all-to-all(bf16[8,128,128]{1,2,0:T(8,128)(2,1)S(1)} %copy.44), channel_id=1, replica_groups={{0,8,16,24,32,40,48,56},{1,9,17,25,33,41,49,57},{2,10,18,26,34,42,50,58..., dimensions={0} | all-to-all | bytes 524288 | tf_op jit(solution)/shard_map/all_to_all | solution.py:117
  264.7 3.1 multiply_reduce_fusion
  269.1 55.4 %all-gather.3 = s32[64,1,128]{2,1,0:T(1,128)S(1)} all-gather(s32[1,1,128]{2,1,0:T(1,128)S(1)} %fusion.39), channel_id=1, replica_groups=mesh['groups'=4,'ctx'=64] {'ctx'}, dimensions={0}, use_global_device_ids=true | all-gather | bytes 33280 | tf_op jit(solution)/shard_map/all_gather | solution.py:138
  324.6 4.9 fusion.49
  329.5 141.9 %all-gather.10.cloned.1.call-done = bf16[8192,2048]{1,0:T(8,128)(2,1)} async-done(((bf16[128,2048]{1,0:T(8,128)(2,1)}), bf16[8192,2048]{1,0:T(8,128)(2,1)}) %all-gather.10.cloned.1.call-update) | async-done | bytes 33554448 | tf_op jit(solution)/shard_map/all_gather | solution.py:139
  471.3 15.6 %convolution_convert_fusion.1 = bf16[64,20,2048]{2,1,0:T(8,128)(2,1)} fusion(bf16[64,128,2048]{2,1,0:T(8,128)(2,1)} %bitcast.62, s32[64,128]{1,0:T(8,128)S(1)} %bitcast.73, s32[20]{0:T(128)S(1)} %iota_add_fusion), kind=kOutput, calls=%fused_computation.2 | convolution fusion | flops 673873920 | bytes 38830160 | tf_op jit(solution)/shard_map/jst,jtw->jsw/dot_general | solution.py:145
  487.0 9.0 %reshape.78 = bf16[1280,2048]{1,0:T(8,128)(2,1)} reshape(bf16[64,20,2048]{2,1,0:T(8,128)(2,1)} %convolution_convert_fusion.1) | data formatting | bytes 10485760 | tf_op jit(solution)/shard_map/reshape | solution.py:147
  496.0 4.0 convolution_reduce_fusion
  500.0 11.7 %fusion.21 = f32[1280,2048]{1,0:T(8,128)} fusion(bf16[512,2048]{1,0:T(8,128)(2,1)} %bitcast.68, bf16[1280,2048]{1,0:T(8,128)(2,1)} %reshape.78, bf16[512,2048]{1,0:T(8,128)(2,1)} %bitcast.67), kind=kOutput, calls=%fused_computation.27 | convolution fusion | flops 5374607360 | bytes 19922944 | tf_op jit(solution)/shard_map/dot_general | solution.py:160
  511.6 11.6 %add_convert_fusion = bf16[1280,2048]{1,0:T(8,128)(2,1)} fusion(f32[1280,2048]{1,0:T(8,128)} %fusion.21, f32[1280]{0:T(1024)S(1)} %add_divide_fusion, bf16[1,512,2048]{2,1,0:T(8,128)(2,1)S(1)} %copy-done, bf16[1280,2048]{1,0:T(8,128)(2,1)} %reshape.78, bf16[1,2048,512]{2,1,0:T(8,128)(2,1)} %param.22), kind=kOutput, calls=%fused_computation.1 | convolution fusion | flops 5382471680 | bytes 25170944 | tf_op jit(solution)/shard_map/dot_general | solution.py:159
  523.3 8.9 %reshape.80 = bf16[64,20,2048]{2,1,0:T(8,128)(2,1)} reshape(bf16[1280,2048]{1,0:T(8,128)(2,1)} %add_convert_fusion) | data formatting | bytes 10485760 | tf_op jit(solution)/shard_map/reshape | solution.py:161
  532.2 16.5 %convolution_convert_fusion = bf16[64,128,2048]{2,1,0:T(8,128)(2,1)} fusion(bf16[64,20,2048]{2,1,0:T(8,128)(2,1)} %reshape.80, s32[64,128]{1,0:T(8,128)S(1)} %bitcast.74, s32[20]{0:T(128)S(1)} %iota_add_fusion), kind=kOutput, calls=%fused_computation | convolution fusion | flops 688029696 | bytes 38830160 | tf_op jit(solution)/shard_map/jst,jsw->jtw/dot_general | solution.py:162
  548.8 258.6 %reduce-scatter.2.cloned.1.call-done = bf16[128,2048]{1,0:T(8,128)(2,1)} async-done(((bf16[8192,2048]{1,0:T(8,128)(2,1)}), bf16[128,2048]{1,0:T(8,128)(2,1)}) %reduce-scatter.2.cloned.1.call-update) | async-done | bytes 524304 | tf_op jit(solution)/shard_map/reduce_scatter | solution.py:164
  807.4 1.9 add_convert_fusion.1
  (30 shorter events, 4.8 us)
Async XLA Ops:
  6.5 505.1 %copy-start = (bf16[1,512,2048]{2,1,0:T(8,128)(2,1)S(1)}, bf16[1,512,2048]{2,1,0:T(8,128)(2,1)}, u32[]{:S(2)}) copy-start(bf16[1,512,2048]{2,1,0:T(8,128)(2,1)} %param.23) | copy-start | bytes 6291460
  6.6 172.3 %all-gather.8.cloned.1.call-start = ((), (), s32[]{:S(2)}) async-start(), calls=%async_computation.4 | async-start | bytes 4718592 | tf_op jit(solution)/shard_map/all_gather | solution.py:109
  119.7 204.8 %all-gather.12.cloned.1.call-start = ((), (), s32[]{:S(2)}) async-start(), calls=%async_computation.6 | async-start | bytes 4718592 | tf_op jit(solution)/shard_map/all_gather | solution.py:112
  121.8 349.6 %all-gather.10.cloned.1.call-start = ((), (), s32[]{:S(2)}) async-start(), calls=%async_computation.5 | async-start | bytes 34078720 | tf_op jit(solution)/shard_map/all_gather | solution.py:139
  264.7 3.2 copy-start.2
  264.7 4.3 copy-start.3
  268.9 538.6 %reduce-scatter.2.cloned.1.call-start = ((), (), s32[]{:S(2)}) async-start(), calls=%async_computation.3 | async-start | bytes 34078720 | tf_op jit(solution)/shard_map/reduce_scatter | solution.py:164
  548.8 260.6 %copy-start.1 = (bf16[1,512,2048]{2,1,0:T(8,128)(2,1)S(1)}, bf16[1,512,2048]{2,1,0:T(8,128)(2,1)}, u32[]{:S(2)}) copy-start(bf16[1,512,2048]{2,1,0:T(8,128)(2,1)} %param.23) | copy-start | bytes 6291460
Sparse Core Ops, SparseCore 0:
  119.9 58.9 all-gather.7
  180.6 86.6 all-gather.11
  269.2 202.0 all-gather.9
  548.9 258.4 reduce-scatter.1

commit v2 on v1

--- a/solution.py
+++ b/solution.py
@@ -13,6 +13,8 @@
 LOG2E = 1.4426950408889634
 KEY_BLOCK = 1024
 QUERY_BLOCK = 256
+HALVES = 2
+SOURCES = 8
 
 
 def attend_kernel(members, tok_rows, q_ref, k_ref, v_ref, o_ref):
@@ -73,6 +75,81 @@
         out_specs=pl.BlockSpec((QUERY_BLOCK, DH), lambda i: (i, 0)),
         cost_estimate=pl.CostEstimate(flops=10**10, bytes_accessed=5 * 10**6, transcendentals=5 * 10**6),
     )(q, k, v)
+
+
+def gelu(x):
+    return x * (0.5 * (1.0 + jnp.tanh(0.7978845608028654 * (x + 0.044715 * (x * x * x)))))
+
+
+def mixture_kernel(
+    token_ref, row_ref, column_ref, router_ref, in_ref, out_ref, up_ref, down_ref, spread_ref, slots
+):
+    block = token_ref.shape[0]
+    pick = lax.broadcasted_iota(jnp.int32, (slots, block), 0) == row_ref[0]
+    pick = jnp.where(pick, 1.0, 0.0).astype(jnp.bfloat16)
+    rows = jnp.dot(pick, token_ref[...], preferred_element_type=jnp.float32)
+    gate = jax.nn.sigmoid(jnp.sum(rows * router_ref[...], axis=1, keepdims=True))
+    rows = rows.astype(jnp.bfloat16)
+    expert_hidden = gelu(
+        jnp.dot(rows, in_ref[...], preferred_element_type=jnp.float32)
+    ).astype(jnp.bfloat16)
+    mlp_hidden = gelu(
+        lax.dot_general(
+            rows, up_ref[...], (((1,), (1,)), ((), ())), preferred_element_type=jnp.float32
+        )
+    ).astype(jnp.bfloat16)
+    produced = gate * jnp.dot(expert_hidden, out_ref[...], preferred_element_type=jnp.float32)
+    produced = produced + jnp.dot(mlp_hidden, down_ref[...], preferred_element_type=jnp.float32)
+    put = lax.broadcasted_iota(jnp.int32, (block, slots), 1) == column_ref[...]
+    put = jnp.where(put, 1.0, 0.0).astype(jnp.bfloat16)
+    spread_ref[...] = jnp.dot(
+        put, produced.astype(jnp.bfloat16), preferred_element_type=jnp.float32
+    ).astype(spread_ref.dtype)
+
+
+def mixture(tokens, local_row, router_row, weight_in, weight_out, up_t, down_t, slots_per):
+    count, width = tokens.shape
+    half_rows = local_row.shape[1]
+    block = SOURCES * half_rows
+    slots = SOURCES * slots_per
+    steps = count // block
+
+    def kernel(*refs):
+        mixture_kernel(*refs, slots)
+
+    def fixed(a):
+        return pl.BlockSpec(a.shape, lambda i: (0, 0))
+
+    return pl.pallas_call(
+        kernel,
+        out_shape=jax.ShapeDtypeStruct((count, width), jnp.bfloat16),
+        grid=(steps,),
+        in_specs=[
+            pl.BlockSpec((block, width), lambda i: (i, 0)),
+            pl.BlockSpec((1, 1, block), lambda i: (i, 0, 0)),
+            pl.BlockSpec((block, 1), lambda i: (i, 0)),
+            fixed(router_row),
+            fixed(weight_in),
+            fixed(weight_out),
+            fixed(up_t),
+            fixed(down_t),
+        ],
+        out_specs=pl.BlockSpec((block, width), lambda i: (i, 0)),
+        cost_estimate=pl.CostEstimate(
+            flops=2 * steps * slots * width * (4 * weight_in.shape[1] + 2 * block),
+            bytes_accessed=4 * count * width + 8 * weight_in.size,
+            transcendentals=2 * steps * slots * weight_in.shape[1],
+        ),
+    )(
+        tokens,
+        local_row.reshape(steps, 1, block),
+        local_row.reshape(count, 1),
+        router_row,
+        weight_in,
+        weight_out,
+        up_t,
+        down_t,
+    )
 
 
 def body(
@@ -125,43 +202,47 @@
     ).astype(jnp.bfloat16)
 
     slots_per = max(2, 5 * tok_rows // (4 * live_count))
+    half_rows = tok_rows // HALVES
     chosen = expert_ids[:, 0]
     onehot = (chosen[:, None] == jnp.arange(live_count, dtype=jnp.int32)[None, :]).astype(
         jnp.bfloat16
     )
     row_iota = jnp.arange(tok_rows, dtype=jnp.int32)
-    strictly_lower = (row_iota[None, :] < row_iota[:, None]).astype(jnp.bfloat16)
-    counts_before = jnp.dot(strictly_lower, onehot, preferred_element_type=jnp.float32)
+    earlier = (row_iota[None, :] < row_iota[:, None]) & (
+        row_iota[None, :] // half_rows == row_iota[:, None] // half_rows
+    )
+    counts_before = jnp.dot(
+        earlier.astype(jnp.bfloat16), onehot, preferred_element_type=jnp.float32
+    )
     slot_index = jnp.sum(onehot.astype(jnp.float32) * counts_before, axis=1).astype(jnp.int32)
     target_slot = chosen * slots_per + slot_index
     own_expert = device_index % live_count
+    tokens = [
+        lax.all_gather(normed[h * half_rows : (h + 1) * half_rows], "ctx", axis=0, tiled=True)
+        for h in range(HALVES)
+    ]
     all_slots = lax.all_gather(target_slot, "ctx", axis=0)
-    tokens = lax.all_gather(normed, "ctx", axis=0)
-    select = (
-        all_slots[:, None, :]
-        == (own_expert * slots_per + jnp.arange(slots_per, dtype=jnp.int32))[None, :, None]
-    ).astype(jnp.bfloat16)
-    rows = (
-        jnp.einsum("jst,jtw->jsw", select, tokens, preferred_element_type=jnp.float32)
-        .astype(jnp.bfloat16)
-        .reshape(-1, width)
-    )
-    router_column = lax.dynamic_slice_in_dim(router, own_expert, 1, 1)
-    weight_in = expert_in[0]
-    weight_out = expert_out[0]
-    expert_hidden = jax.nn.gelu(
-        jnp.dot(rows, weight_in, preferred_element_type=jnp.float32)
-    ).astype(jnp.bfloat16)
-    mlp_hidden = jax.nn.gelu(
-        lax.dot_general(rows, up_t, (((1,), (1,)), ((), ())), preferred_element_type=jnp.float32)
-    ).astype(jnp.bfloat16)
-    gate = jax.nn.sigmoid(jnp.dot(rows, router_column, preferred_element_type=jnp.float32))
-    produced = gate * jnp.dot(expert_hidden, weight_out, preferred_element_type=jnp.float32)
-    produced = produced + jnp.dot(mlp_hidden, down_t, preferred_element_type=jnp.float32)
-    produced = produced.astype(jnp.bfloat16).reshape(ctx_count, slots_per, width)
-    spread = jnp.einsum("jst,jsw->jtw", select, produced, preferred_element_type=jnp.float32)
-    spread = spread.astype(jnp.bfloat16).reshape(ctx_count * tok_rows, width)
-    summed = lax.psum_scatter(spread, "ctx", scatter_dimension=0, tiled=True)
+    local_slot = all_slots - own_expert * slots_per
+    source = jnp.arange(ctx_count, dtype=jnp.int32)[:, None] % SOURCES
+    local_row = jnp.where(
+        (local_slot >= 0) & (local_slot < slots_per), source * slots_per + local_slot, -1
+    )
+    router_row = lax.dynamic_slice_in_dim(router, own_expert, 1, 1).T.astype(jnp.float32)
+    summed = []
+    for h in range(HALVES):
+        rows_here = local_row[:, h * half_rows : (h + 1) * half_rows]
+        spread = mixture(
+            tokens[h],
+            rows_here,
+            router_row,
+            expert_in[0],
+            expert_out[0],
+            up_t,
+            down_t,
+            slots_per,
+        )
+        summed.append(lax.psum_scatter(spread, "ctx", scatter_dimension=0, tiled=True))
+    summed = jnp.concatenate(summed, axis=0)
     return (mixed + summed.astype(jnp.float32)).astype(jnp.bfloat16)
 
 

time: 817 us -> 1030 us (1.26)
  waiting for transfers between devices: 457 us -> 680 us
  matrix products: 62.8 us -> 3.24 us
  Pallas kernels: 16.2 us -> 74.6 us
    reduce_scatter x1 -> x2, waiting for transfers between devices: 259 us -> 433 us  [body(): lax.psum_scatter(spread, 'ctx', scatter_dimension=0, tiled=True)]
    dot_general x6 -> x1, matrix products: 59.6 us -> 0.22 us  [body(): jnp.dot(earlier.astype(jnp.bfloat16), onehot, preferred_element_type=jnp....]
    pallas_call x0 -> x2, Pallas kernels: none -> 58.4 us  [mixture(): pl.pallas_call(kernel, out_shape=jax.ShapeDtypeStruct((count, width), jnp...]
    all_gather x1 -> x2, waiting for transfers between devices: 142 us -> 190 us  [body(): lax.all_gather(normed[h * half_rows:(h + 1) * half_rows], 'ctx', axis=0,...]
  transfers between devices with their start and end apart: 4 -> 6, of which waited for: 3 -> 5; matrix products, arithmetic and copies ran while one was open for 2% -> 3% of each run, Pallas kernels for 2% -> 7%
where the time goes in v2:
time: 1030 us
  waiting for transfers between devices  680 us (66%)
  blocking collectives  226 us (22%)
  Pallas kernels  74.6 us (7%)
  local copies, waits for them, and re-layouts  26.5 us (3%)
  between operations  13.7 us (1%)
    reduce_scatter x2, waiting for transfers between devices, body(): lax.psum_scatter(spread, 'ctx', scatter_dimension=0, tiled=True)  433 us
    all_gather x2, waiting for transfers between devices, body(): lax.all_gather(normed[h * half_rows:(h + 1) * half_rows], 'ctx', axis=0,...  190 us
    all_to_all x1, blocking collectives, body(): lax.all_to_all(qkv, 'ctx', split_axis=0, concat_axis=0, tiled=True, axis_...  108 us
    all_to_all x1, blocking collectives, body(): lax.all_to_all(o, 'ctx', split_axis=0, concat_axis=0, tiled=True, axis_in...  62.6 us
    pallas_call x2, Pallas kernels, mixture(): pl.pallas_call(kernel, out_shape=jax.ShapeDtypeStruct((count, width), jnp...  58.4 us
    all_gather x1, waiting for transfers between devices, body(): kv = lax.all_gather(mine[:, 1:], 'ctx', axis=0, axis_index_groups=within)  57.2 us
    all_gather x1, blocking collectives, body(): all_slots = lax.all_gather(target_slot, 'ctx', axis=0)  54.6 us
  transfers between devices with their start and end apart: 6, of which 5 were waited for; matrix products, arithmetic and copies ran while one was open for 3% of the time, Pallas kernels for 7%

profile of v2, /device:TPU:38, one launch (start us, length us, event | category | flops | bytes accessed | tf_op | source)
XLA Modules:
  0.0 1029.1 jit_solution(5239857796662084493)
XLA Ops:
  6.6 1.1 copy.50
  7.7 1.1 copy.51
  8.8 1.1 copy.52
  10.1 108.5 %all_to_all.10 = bf16[8,3,128,128]{2,3,1,0:T(8,128)(2,1)S(1)} all-to-all(bf16[8,3,128,128]{2,3,1,0:T(8,128)(2,1)S(1)} %copy.53), channel_id=1, replica_groups={{0,8,16,24,32,40,48,56},{1,9,17,25,33,41,49,57},{2,10,18,26,34,42,50,58..., dimensions={0} | all-to-all | bytes 1572864 | tf_op jit(solution)/shard_map/all_to_all | solution.py:182
  121.7 57.2 %all-gather.12.cloned.1.call-done = bf16[64,2,128,128]{3,2,1,0:T(8,128)(2,1)} async-done(((bf16[8,2,128,128]{3,2,1,0:T(8,128)(2,1)}), bf16[64,2,128,128]{3,2,1,0:T(8,128)(2,1)}) %all-gather.12.cloned.1.call-update) | async-done | bytes 4194320 | tf_op jit(solution)/shard_map/all_gather | solution.py:186
  178.8 2.7 slice_bitcast_fusion
  181.6 1.6 copy.57
  183.2 1.6 copy.56
  184.7 16.2 %shard_map.118 = bf16[1024,128]{1,0:T(8,128)(2,1)} custom-call(bf16[1024,128]{1,0:T(8,128)(2,1)} %bitcast.65, bf16[8192,128]{1,0:T(8,128)(2,1)} %bitcast.56, bf16[8192,128]{1,0:T(8,128)(2,1)} %bitcast.55), custom_call_target="tpu_custom_call" | custom-call | flops 10000000000 | bytes 5000000 | tf_op jit(solution)/shard_map/pallas_call | solution.py:70
  201.0 1.1 copy.58
  202.1 62.6 %all_to_all.11 = bf16[8,128,128]{1,2,0:T(8,128)(2,1)S(1)} all-to-all(bf16[8,128,128]{1,2,0:T(8,128)(2,1)S(1)} %copy.58), channel_id=1, replica_groups={{0,8,16,24,32,40,48,56},{1,9,17,25,33,41,49,57},{2,10,18,26,34,42,50,58..., dimensions={0} | all-to-all | bytes 524288 | tf_op jit(solution)/shard_map/all_to_all | solution.py:194
  264.8 3.0 multiply_reduce_fusion
  269.9 54.6 %all-gather.2 = s32[64,1,128]{2,1,0:T(1,128)S(1)} all-gather(s32[1,1,128]{2,1,0:T(1,128)S(1)} %fusion.9), channel_id=1, replica_groups=mesh['groups'=4,'ctx'=64] {'ctx'}, dimensions={0}, use_global_device_ids=true | all-gather | bytes 33280 | tf_op jit(solution)/shard_map/all_gather | solution.py:224
  324.7 3.4 reshape.183.refs_2_
  328.8 1.4 bitcast_convert_fusion.refs_3_
  330.2 5.0 fusion.10
  335.1 81.1 %all-gather.8.cloned.1.call-done.refs_0_ = bf16[4096,2048]{1,0:T(8,128)(2,1)} async-done(((bf16[64,2048]{1,0:T(8,128)(2,1)}), bf16[4096,2048]{1,0:T(8,128)(2,1)}) %all-gather.8.cloned.1.call-update) | async-done | bytes 16777232 | tf_op jit(solution)/shard_map/all_gather | solution.py:221
  416.3 29.2 %shard_map.119 = bf16[4096,2048]{1,0:T(8,128)(2,1)} custom-call(bf16[4096,2048]{1,0:T(8,128)(2,1)} %all-gather.8.cloned.1.call-done.refs_0_, s32[8,1,512]{2,1,0:T(1,128)} %reshape.172.refs_1_, s32[4096,1]{1,0:T(8,128)} %reshape.183.refs_2_, f32[1,2048]{1,0:T(1,128)} %bitcast_convert_fusion.refs_3_, bf16[2048,512]{1,0:T(8,128)(2,1)} %bitcast.71, ...), custom_call_target="tpu_custom_call" | custom-call | flops 16106127360 | bytes 41943040 | tf_op jit(solution)/shard_map/pallas_call | solution.py:123
  445.7 3.4 reshape.184.refs_2_
  449.8 108.5 %all-gather.10.cloned.1.call-done.refs_0_ = bf16[4096,2048]{1,0:T(8,128)(2,1)} async-done(((bf16[64,2048]{1,0:T(8,128)(2,1)}), bf16[4096,2048]{1,0:T(8,128)(2,1)}) %all-gather.10.cloned.1.call-update) | async-done | bytes 16777232 | tf_op jit(solution)/shard_map/all_gather | solution.py:221
  558.4 29.2 %shard_map.120 = bf16[4096,2048]{1,0:T(8,128)(2,1)} custom-call(bf16[4096,2048]{1,0:T(8,128)(2,1)} %all-gather.10.cloned.1.call-done.refs_0_, s32[8,1,512]{2,1,0:T(1,128)} %reshape.174.refs_1_, s32[4096,1]{1,0:T(8,128)} %reshape.184.refs_2_, f32[1,2048]{1,0:T(1,128)} %bitcast_convert_fusion.refs_3_, bf16[2048,512]{1,0:T(8,128)(2,1)} %bitcast.72, ...), custom_call_target="tpu_custom_call" | custom-call | flops 16106127360 | bytes 41943040 | tf_op jit(solution)/shard_map/pallas_call | solution.py:123
  587.7 198.2 %reduce-scatter.3.cloned.1.call-done = bf16[64,2048]{1,0:T(8,128)(2,1)} async-done(((bf16[4096,2048]{1,0:T(8,128)(2,1)}), bf16[64,2048]{1,0:T(8,128)(2,1)}) %reduce-scatter.3.cloned.1.call-update) | async-done | bytes 262160 | tf_op jit(solution)/shard_map/reduce_scatter | solution.py:244
  785.9 234.4 %reduce-scatter.5.cloned.1.call-done = bf16[64,2048]{1,0:T(8,128)(2,1)} async-done(((bf16[4096,2048]{1,0:T(8,128)(2,1)}), bf16[64,2048]{1,0:T(8,128)(2,1)}) %reduce-scatter.5.cloned.1.call-update) | async-done | bytes 262160 | tf_op jit(solution)/shard_map/reduce_scatter | solution.py:244
  1020.3 1.9 add_convert_fusion
  (42 shorter events, 7.1 us)
Async XLA Ops:
  6.5 172.3 %all-gather.12.cloned.1.call-start = ((), (), s32[]{:S(2)}) async-start(), calls=%async_computation.8 | async-start | bytes 4718592 | tf_op jit(solution)/shard_map/all_gather | solution.py:186
  10.1 109.7 %copy-start.1 = (bf16[2048,64]{0,1:T(8,128)(2,1)S(1)}, bf16[2048,64]{0,1:T(8,128)(2,1)}, u32[]{:S(2)}) copy-start(bf16[2048,64]{0,1:T(8,128)(2,1)} %param.19) | copy-start | bytes 786436
  10.1 109.7 %copy-start.2 = (bf16[2048,64]{0,1:T(8,128)(2,1)S(1)}, bf16[2048,64]{0,1:T(8,128)(2,1)}, u32[]{:S(2)}) copy-start(bf16[2048,64]{0,1:T(8,128)(2,1)} %param.18) | copy-start | bytes 786436
  119.7 210.4 %all-gather.14.cloned.1.call-start = ((), (), s32[]{:S(2)}) async-start(), calls=%async_computation.9 | async-start | bytes 4718592 | tf_op jit(solution)/shard_map/all_gather | solution.py:189
  120.7 295.5 %all-gather.8.cloned.1.call-start = ((), (), s32[]{:S(2)}) async-start(), calls=%async_computation.4 | async-start | bytes 17039360 | tf_op jit(solution)/shard_map/all_gather | solution.py:221
  184.7 80.0 %copy-start = (bf16[128,2048]{1,0:T(8,128)(2,1)S(1)}, bf16[128,2048]{1,0:T(8,128)(2,1)}, u32[]{:S(2)}) copy-start(bf16[128,2048]{1,0:T(8,128)(2,1)} %param.15) | copy-start | bytes 1572868
  264.7 3.0 copy-start.3
  267.8 1.9 copy-start.4
  268.9 289.5 %all-gather.10.cloned.1.call-start = ((), (), s32[]{:S(2)}) async-start(), calls=%async_computation.6 | async-start | bytes 17039360 | tf_op jit(solution)/shard_map/all_gather | solution.py:221
  269.5 516.3 %reduce-scatter.3.cloned.1.call-start = ((), (), s32[]{:S(2)}) async-start(), calls=%async_computation.5 | async-start | bytes 17039360 | tf_op jit(solution)/shard_map/reduce_scatter | solution.py:244
  445.5 574.8 %reduce-scatter.5.cloned.1.call-start = ((), (), s32[]{:S(2)}) async-start(), calls=%async_computation.7 | async-start | bytes 17039360 | tf_op jit(solution)/shard_map/reduce_scatter | solution.py:244
Sparse Core Ops, SparseCore 0:
  119.8 58.9 all-gather.11
  180.6 86.6 all-gather.13
  269.2 146.9 all-gather.7
  418.0 140.3 all-gather.9
  560.8 225.0 reduce-scatter.2
  788.3 231.9 reduce-scatter.4
